TPU v7x, 32 devices: a whole 2x2x4 slice. The times are simulated.
32 devices in a mesh: dp: 8 (over y, x, core), mp: 4 (over z).
Axes of the slice: x: 2, y: 2, z: 4, core: 2. Of those that a mesh axis runs over, the one named last changes fastest.
Arguments:
- hidden: bfloat16 [64, 4096], P('dp'), may hold values from -6 to 6
- attention_gain: float32 [4096], replicated, may hold values from 0.5 to 1.5
- query_weight: bfloat16 [4096, 4096], P(None, 'mp'), may hold values from -0.09375 to 0.09375
- key_weight: bfloat16 [4096, 1024], P(None, 'mp'), may hold values from -0.09375 to 0.09375
- value_weight: bfloat16 [4096, 1024], P(None, 'mp'), may hold values from -0.09375 to 0.09375
- output_weight: bfloat16 [4096, 4096], P('mp'), may hold values from -0.09375 to 0.09375
- key_cache: bfloat16 [64, 8, 4096, 128], P('dp', 'mp'), may hold values from -9 to 9
- value_cache: bfloat16 [64, 8, 4096, 128], P('dp', 'mp'), may hold values from -8 to 8, as said below
- lengths: int32 [64], P('dp'), may hold values from 128 to 4096, as said below
- finished: int32 [64], P('dp'), may hold values 0 or 1
- feed_gain: float32 [4096], replicated, may hold values from 0.5 to 1.5
- gate_weight: bfloat16 [4096, 14336], P(None, ('dp', 'mp')), may hold values from -0.09375 to 0.09375
- up_weight: bfloat16 [4096, 14336], P(None, ('dp', 'mp')), may hold values from -0.09375 to 0.09375
- down_weight: bfloat16 [14336, 4096], P(('dp', 'mp')), may hold values from -0.046875 to 0.046875
- final_gain: float32 [4096], replicated, may hold values from 0.5 to 8, as said below
- vocab_weight: bfloat16 [4096, 128256], P(None, ('dp', 'mp')), may hold values from -0.375 to 0.375
- next_tokens: int32 [64], replicated, may hold values from 0 to 128255
Outputs:
- log_likelihood: float32 [64], P('dp')
Inputs may be any that keep to these rules, and one draw needn't show every extreme that they name: `lengths`: each rollout has 128 to 4096 cached tokens; both ends are reached in every draw; rollouts held by one index of dp share a length scale, so devices' total cached tokens differ. `finished`: 0 or 1. `next_tokens`: a vocabulary entry. `value_cache`: a per-rollout and per-head mean plus noise. `final_gain`: positive gains.
All inputs are finite; a program needn't handle non-finite values.
Results may differ from a plain program's by a relative error of at most 0.0055.
Values may be sent and summed in bfloat16 or wider, within the bound.
A program may use at most 192 MiB of HBM per device.

v0:
```python
import math
import jax
import jax.numpy as jnp
from jax import lax
from jax.sharding import PartitionSpec as P

H = 32
KVH = 8
EPSILON = 1e-05
THETA = 500000.0
NEGATIVE = -1e30


def joined(value, axis, join):
    pieces = jax.tree.map(lambda part: lax.all_gather(part, axis), value)
    head = jax.tree.map(lambda part: part[0], pieces)
    tail = jax.tree.map(lambda part: part[1:], pieces)
    subtotal, _ = lax.scan(lambda subtotal, piece: (join(subtotal, piece), None), head, tail)
    return subtotal


def rms_norm(hidden, gain):
    wide = hidden.astype(jnp.float32)
    scale = lax.rsqrt(jnp.mean(wide * wide, axis=-1, keepdims=True) + EPSILON)
    return (wide * scale * gain).astype(jnp.bfloat16)


def rotate(heads, positions):
    half = heads.shape[-1] // 2
    exponent = jnp.arange(half, dtype=jnp.float32) * (-2.0 / heads.shape[-1])
    frequency = jnp.power(jnp.float32(THETA), exponent)
    angles = positions.astype(jnp.float32)[:, None, None] * frequency[None, None, :]
    cosine = jnp.cos(angles)
    sine = jnp.sin(angles)
    former = heads[..., :half]
    latter = heads[..., half:]
    return jnp.concatenate(
        [former * cosine - latter * sine, latter * cosine + former * sine], axis=-1
    )


def combine_parts(former, latter):
    highest = jnp.maximum(former[0], latter[0])
    spread = former[1] * jnp.exp(former[0] - highest) + latter[1] * jnp.exp(latter[0] - highest)
    return (highest, spread, former[2] + latter[2])


def padded_attention(queries, own, key_cache, value_cache, new_values, lengths):
    head_width = queries.shape[-1]
    scale = 1.0 / math.sqrt(head_width)
    scores = (
        jnp.einsum("rkgd,rkld->rkgl", queries, key_cache, preferred_element_type=jnp.float32)
        * scale
    )
    places = lax.broadcasted_iota(jnp.int32, (1, 1, 1, key_cache.shape[2]), 3)
    scores = jnp.where(places < lengths[:, None, None, None], scores, NEGATIVE)
    top = jnp.maximum(jnp.max(scores, axis=-1), own)
    weights = jnp.exp(scores - top[..., None])
    own_weight = jnp.exp(own - top)
    total = jnp.sum(weights, axis=-1) + own_weight
    mixed = jnp.einsum(
        "rkgl,rkld->rkgd",
        weights.astype(jnp.bfloat16),
        value_cache,
        preferred_element_type=jnp.float32,
    )
    mixed = mixed + own_weight[..., None] * new_values.astype(jnp.float32)[:, :, None, :]
    return (mixed / total[..., None]).astype(jnp.bfloat16)


def shards(
    hidden,
    attention_gain,
    query_weight,
    key_weight,
    value_weight,
    output_weight,
    key_cache,
    value_cache,
    lengths,
    finished,
    feed_gain,
    gate_weight,
    up_weight,
    down_weight,
    final_gain,
    vocab_weight,
    next_tokens,
):
    local_rows = hidden.shape[0]
    key_heads = key_cache.shape[1]
    head_width = key_cache.shape[3]
    groups = H // KVH
    normed = rms_norm(hidden, attention_gain)
    queries = jnp.dot(normed, query_weight, preferred_element_type=jnp.float32).reshape(
        local_rows, key_heads * groups, head_width
    )
    queries = (
        rotate(queries, lengths)
        .astype(jnp.bfloat16)
        .reshape(local_rows, key_heads, groups, head_width)
    )
    new_keys = jnp.dot(normed, key_weight, preferred_element_type=jnp.float32).reshape(
        local_rows, key_heads, head_width
    )
    new_keys = rotate(new_keys, lengths).astype(jnp.bfloat16)
    new_values = (
        jnp.dot(normed, value_weight, preferred_element_type=jnp.float32)
        .astype(jnp.bfloat16)
        .reshape(local_rows, key_heads, head_width)
    )
    own = jnp.einsum("rkgd,rkd->rkg", queries, new_keys, preferred_element_type=jnp.float32) * (
        1.0 / math.sqrt(head_width)
    )
    attended = padded_attention(queries, own, key_cache, value_cache, new_values, lengths)
    partial_heads = jnp.dot(
        attended.reshape(local_rows, key_heads * groups * head_width),
        output_weight,
        preferred_element_type=jnp.float32,
    )
    attention = lax.psum(partial_heads.astype(jnp.bfloat16), "mp").astype(jnp.float32)
    mixed_hidden = (hidden.astype(jnp.float32) + attention).astype(jnp.bfloat16)
    feed_in = rms_norm(mixed_hidden, feed_gain)

    def activate(piece):
        gate = jnp.dot(piece, gate_weight, preferred_element_type=jnp.float32)
        upward = jnp.dot(piece, up_weight, preferred_element_type=jnp.float32)
        return (jax.nn.silu(gate) * upward).astype(jnp.bfloat16)

    activation = activate(lax.all_gather(feed_in, "dp", axis=0, tiled=True))
    partial_feed = lax.psum_scatter(
        jnp.dot(
            lax.slice_in_dim(activation, 0, local_rows * lax.axis_size("dp"), axis=0),
            down_weight,
            preferred_element_type=jnp.float32,
        ).astype(jnp.bfloat16),
        "dp",
        scatter_dimension=0,
        tiled=True,
    ).astype(jnp.float32)
    feed = lax.psum(partial_feed.astype(jnp.bfloat16), "mp").astype(jnp.float32)
    residual = (mixed_hidden.astype(jnp.float32) + feed).astype(jnp.bfloat16)
    final = rms_norm(residual, final_gain)

    def score_rows(piece):
        return jnp.dot(piece, vocab_weight, preferred_element_type=jnp.float32)

    logits = score_rows(lax.all_gather(final, "dp", axis=0, tiled=True))
    vocab_local = vocab_weight.shape[1]
    vocab_start = (lax.axis_index("dp") * lax.axis_size("mp") + lax.axis_index("mp")) * vocab_local
    offsets = next_tokens - vocab_start
    matches = lax.broadcasted_iota(jnp.int32, (1, vocab_local), 1) == offsets[:, None]
    picked = jnp.sum(jnp.where(matches, logits, 0.0), axis=-1)
    local_top = jnp.max(logits, axis=-1)
    local_spread = jnp.sum(jnp.exp(logits - local_top[:, None]), axis=-1)
    top, spread_sum, picked = joined((local_top, local_spread, picked), ("dp", "mp"), combine_parts)
    normalizer = top + jnp.log(spread_sum)
    row_start = lax.axis_index("dp") * local_rows
    chosen = lax.dynamic_slice_in_dim(picked - normalizer, row_start, local_rows, 0)
    return jnp.where(finished != 0, 0.0, chosen).astype(jnp.float32)


def solution(mesh):
    in_specs = (
        P("dp", None),
        P(),
        P(None, "mp"),
        P(None, "mp"),
        P(None, "mp"),
        P("mp", None),
        P("dp", "mp", None, None),
        P("dp", "mp", None, None),
        P("dp"),
        P("dp"),
        P(),
        P(None, ("dp", "mp")),
        P(None, ("dp", "mp")),
        P(("dp", "mp"), None),
        P(),
        P(None, ("dp", "mp")),
        P(),
    )
    out_specs = P("dp")
    return jax.shard_map(shards, mesh=mesh, in_specs=in_specs, out_specs=out_specs, check_vma=False)
```

profile of v0, /device:TPU:0, one launch (start us, length us, event | category | flops | bytes accessed | tf_op | source)
XLA Modules:
  0.0 245.2 jit_solution(16923036715946141250)
XLA Ops:
  6.6 0.8 convert_element_type.71
  7.4 0.7 iota_compare_fusion.1
  8.1 1.0 fusion.20
  9.1 1.3 convolution_bitcast_fusion.1
  10.4 4.7 %convolution_bitcast_fusion = f32[8,8,128]{2,0,1:T(8,128)S(1)} fusion(bf16[4096,1024]{1,0:T(8,128)(2,1)} %param.21, bf16[8,4096]{1,0:T(8,128)(2,1)} %param.19, f32[4096]{0:T(1024)} %param.20, f32[8]{0:T(128)S(1)} %add_rsqrt_fusion.2), kind=kOutput, calls=%fused_computation.18 | convolution fusion | flops 67239936 | bytes 8503328 | tf_op jit(solution)/shard_map/dot_general | solution.py:95
  15.0 0.1 multiply_cosine_fusion
  15.1 0.1 subtract_convert_fusion.1
  15.2 0.1 subtract_convert_fusion
  15.3 0.1 maximum_bitcast_fusion
  15.4 0.2 fusion.34
  15.6 0.0 copy-start.3
  15.6 10.4 %fusion.43 = (f32[8,2,4]{2,1,0:T(2,128)S(1)}, f32[8,2,4,4096]{3,2,1,0:T(4,128)S(1)}) fusion(bf16[8,2,4096,128]{3,2,1,0:T(8,128)(2,1)} %param.25, bf16[8,2,4,64]{3,2,1,0:T(4,128)(2,1)S(1)} %bitcast.51, bf16[8,2,4,64]{3,2,1,0:T(4,128)(2,1)S(1)} %bitcast.49, pred[8,4096]{1,0:T(8,128)(4,1)S(1)} %iota_compare_fusion.1), kind=kOutput, calls=%fused_computation.78 | convolution fusion | flops 67928000 | bytes 17875200 | tf_op jit(solution)/shard_map/rkgd,rkld->rkgl/dot_general | solution.py:52
  26.0 0.5 fusion.13
  26.6 2.0 fusion.12
  28.6 7.1 %fusion.10 = bf16[8,2,4,128]{3,2,1,0:T(4,128)(2,1)S(1)} fusion(bf16[8,2,4096,128]{3,2,1,0:T(8,128)(2,1)} %param.26, f32[8,2,4,4096]{3,2,1,0:T(4,128)S(1)} %get-tuple-element.80, f32[8,2,4]{2,1,0:T(2,128)S(1)} %multiply_maximum_fusion, f32[8,2,4]{2,1,0:T(2,128)S(1)} %get-tuple-element.70, f32[8,2,128]{2,1,0:T(2,128)S(1)} %copy.20, ...), kind=kOutput, calls=%fused_computation.19 | convolution fusion | flops 67665920 | bytes 17851136 | tf_op jit(solution)/shard_map/rkgl,rkld->rkgd/dot_general | solution.py:61
  35.7 0.0 copy-start.4
  35.7 5.2 %convolution_convert_fusion.1 = bf16[8,4096]{1,0:T(8,128)(2,1)} fusion(bf16[8,1024]{1,0:T(8,128)(2,1)S(1)} %reshape.136, bf16[1024,4096]{1,0:T(8,128)(2,1)} %param.24), kind=kOutput, calls=%fused_computation.13 | convolution fusion | flops 67141632 | bytes 8470528 | tf_op jit(solution)/shard_map/dot_general | solution.py:116
  40.9 0.0 all-reduce.7.cloned.1.call-update
  40.9 0.0 reduce-scatter.2.cloned.1.call-start
  41.0 37.1 %all-reduce.7.cloned.1.call-done = bf16[8,4096]{1,0:T(8,128)(2,1)} async-done(((bf16[8,4096]{1,0:T(8,128)(2,1)}), bf16[8,4096]{1,0:T(8,128)(2,1)}) %all-reduce.7.cloned.1.call-update) | async-done | bytes 65552 | tf_op jit(solution)/shard_map/psum | solution.py:121
  78.1 1.0 fusion.24
  79.1 0.1 fusion.26
  79.2 9.8 %all_gather.24 = bf16[64,4096]{1,0:T(8,128)(2,1)S(1)} all-gather(bf16[8,4096]{1,0:T(8,128)(2,1)S(1)} %fusion.26), channel_id=1, replica_groups=mesh['dp'=8,'mp'=4] {'dp'}, dimensions={0}, use_global_device_ids=true | all-gather | bytes 589824 | tf_op jit(solution)/shard_map/all_gather | solution.py:130
  89.0 3.2 %fusion.45 = f32[64,448]{1,0:T(8,128)S(1)} fusion(bf16[64,4096]{1,0:T(8,128)(2,1)S(1)} %all_gather.24, bf16[4096,448]{0,1:T(8,128)(2,1)} %param.30), kind=kOutput, calls=%fused_computation.80 | convolution fusion | flops 234881024 | bytes 4308992 | tf_op jit(solution)/shard_map/dot_general | solution.py:126
  92.2 0.0 copy-start.5
  92.2 6.1 %convolution_convert_fusion = bf16[64,4096]{1,0:T(8,128)(2,1)} fusion(bf16[448,4096]{1,0:T(8,128)(2,1)} %param.32, bf16[64,4096]{1,0:T(8,128)(2,1)S(1)} %all_gather.24, bf16[4096,448]{0,1:T(8,128)(2,1)} %param.31, f32[64,448]{1,0:T(8,128)S(1)} %fusion.45), kind=kOutput, calls=%fused_computation.12 | convolution fusion | flops 470196224 | bytes 8503296 | tf_op jit(solution)/shard_map/dot_general | solution.py:132
  98.3 0.0 reduce-scatter.2.cloned.1.call-update
  98.4 0.0 all-reduce.9.cloned.1.call-start
  98.4 33.0 %reduce-scatter.2.cloned.1.call-done = bf16[8,4096]{1,0:T(8,128)(2,1)} async-done(((bf16[64,4096]{1,0:T(8,128)(2,1)}), bf16[8,4096]{1,0:T(8,128)(2,1)}) %reduce-scatter.2.cloned.1.call-update) | async-done | bytes 65552 | tf_op jit(solution)/shard_map/reduce_scatter | solution.py:131
  131.4 0.0 all-reduce.9.cloned.1.call-update
  131.5 36.6 %all-reduce.9.cloned.1.call-done = bf16[8,4096]{1,0:T(8,128)(2,1)} async-done(((bf16[8,4096]{1,0:T(8,128)(2,1)}), bf16[8,4096]{1,0:T(8,128)(2,1)}) %all-reduce.9.cloned.1.call-update) | async-done | bytes 65552 | tf_op jit(solution)/shard_map/psum | solution.py:141
  168.1 1.0 fusion.17
  169.1 0.9 fusion.19
  170.0 10.0 %all_gather.25 = bf16[64,4096]{1,0:T(8,128)(2,1)S(1)} all-gather(bf16[8,4096]{1,0:T(8,128)(2,1)S(1)} %fusion.19), channel_id=1, replica_groups=mesh['dp'=8,'mp'=4] {'dp'}, dimensions={0}, use_global_device_ids=true | all-gather | bytes 589824 | tf_op jit(solution)/shard_map/all_gather | solution.py:148
  180.0 15.6 %fusion.44 = (f32[64]{0:T(128)S(1)}, f32[64,4008]{1,0:T(8,128)S(1)}) fusion(bf16[64,4096]{1,0:T(8,128)(2,1)S(1)} %all_gather.25, bf16[4096,4008]{0,1:T(8,128)(2,1)} %param.34), kind=kOutput, calls=%fused_computation.79 | convolution fusion | flops 2101602816 | bytes 34384128 | tf_op jit(solution)/shard_map/dot_general | solution.py:146
  195.6 0.5 select_reduce_fusion
  196.1 0.3 dynamic-update-slice
  196.4 0.3 dynamic-update-slice.2
  196.6 0.3 dynamic-update-slice.1
  196.9 39.4 %all-reduce.3 = (f32[2048]{0:T(1024)S(1)}, f32[2048]{0:T(1024)S(1)}, f32[2048]{0:T(1024)S(1)}) all-reduce(f32[2048]{0:T(1024)S(1)} %dynamic-update-slice, f32[2048]{0:T(1024)S(1)} %dynamic-update-slice.1, f32[2048]{0:T(1024)S(1)} %dynamic-update-slice.2), channel_id=2, replica_groups=mesh['dp'=8,'mp'=4] {'dp','mp'}, use_global_device_ids=true, to_apply=%add | all-reduce | flops 6144 | bytes 49152
  236.3 0.1 slice.53
  236.3 0.1 slice.54
  236.4 0.1 slice.55
  236.5 0.1 reshape.147
  236.6 0.1 reshape.148
  236.6 0.1 reshape.149
  236.7 1.4 while.14
  238.1 0.6 compare_select_fusion
  (63 shorter events, 1.1 us)
Async XLA Ops:
  6.5 2.6 %copy-start = (bf16[4096,256]{1,0:T(8,128)(2,1)S(1)}, bf16[4096,256]{1,0:T(8,128)(2,1)}, u32[]{:S(2)}) copy-start(bf16[4096,256]{1,0:T(8,128)(2,1)} %param.22) | copy-start | bytes 6291460
  6.5 71.6 %all-reduce.7.cloned.1.call-start = ((), (), s32[]{:S(2)}) async-start(), calls=%async_computation.1 | async-start | bytes 131072 | tf_op jit(solution)/shard_map/psum | solution.py:121
  15.6 10.9 %copy-start.2 = (bf16[8,4096]{1,0:T(8,128)(2,1)S(1)}, bf16[8,4096]{1,0:T(8,128)(2,1)}, u32[]{:S(2)}) copy-start(bf16[8,4096]{1,0:T(8,128)(2,1)} %param.19) | copy-start | bytes 196612
  15.6 10.9 %copy-start.3 = (f32[4096]{0:T(1024)S(1)}, f32[4096]{0:T(1024)}, u32[]{:S(2)}) copy-start(f32[4096]{0:T(1024)} %param.20) | copy-start | bytes 49156
  35.7 43.4 %copy-start.4 = (f32[4096]{0:T(1024)S(1)}, f32[4096]{0:T(1024)}, u32[]{:S(2)}) copy-start(f32[4096]{0:T(1024)} %param.29) | copy-start | bytes 49156
  40.9 90.5 %reduce-scatter.2.cloned.1.call-start = ((), (), s32[]{:S(2)}) async-start(), calls=%async_computation.2 | async-start | bytes 589824 | tf_op jit(solution)/shard_map/reduce_scatter | solution.py:131
  92.2 39.2 %copy-start.7 = (s32[64]{0:T(128)S(1)}, s32[64]{0:T(128)}, u32[]{:S(2)}) copy-start(s32[64]{0:T(128)} %param.35) | copy-start | bytes 772
  92.2 76.9 %copy-start.5 = (f32[4096]{0:T(1024)S(1)}, f32[4096]{0:T(1024)}, u32[]{:S(2)}) copy-start(f32[4096]{0:T(1024)} %param.33) | copy-start | bytes 49156
  98.4 69.7 %all-reduce.9.cloned.1.call-start = ((), (), s32[]{:S(2)}) async-start(), calls=%async_computation.3 | async-start | bytes 131072 | tf_op jit(solution)/shard_map/psum | solution.py:141
  180.0 58.1 %copy-start.6 = (s32[8]{0:T(128)S(1)}, s32[8]{0:T(128)}, u32[]{:S(2)}) copy-start(s32[8]{0:T(128)} %param.28) | copy-start | bytes 100
  180.0 58.7 %copy-start.1 = (bf16[4096,256]{1,0:T(8,128)(2,1)S(1)}, bf16[4096,256]{1,0:T(8,128)(2,1)}, u32[]{:S(2)}) copy-start(bf16[4096,256]{1,0:T(8,128)(2,1)} %param.22) | copy-start | bytes 6291460
Sparse Core Ops, SparseCore 0:
  41.1 37.0 all-reduce.6
  98.5 32.9 reduce-scatter.1
  133.8 34.2 all-reduce.8
where the time goes:
time: 246 us; the launch traced here: 245 us
  waiting for transfers between devices  107 us (43%)
  blocking collectives  59.2 us (24%)
  matrix products  55.7 us (23%)
  between operations  13.3 us (5%)
  other arithmetic  8.45 us (3%)
    unnamed x1, blocking collectives  39.4 us
    psum x1, waiting for transfers between devices, shards(): lax.psum(partial_heads.astype(jnp.bfloat16), 'mp').astype(jnp.float32)  37.1 us
    psum x1, waiting for transfers between devices, shards(): feed = lax.psum(partial_feed.astype(jnp.bfloat16), 'mp').astype(jnp.float32)  36.6 us
    reduce_scatter x1, waiting for transfers between devices, shards(): lax.psum_scatter(jnp.dot(lax.slice_in_dim(activation, 0, local_rows * lax...  33 us
    dot_general x1, matrix products, score_rows(): return jnp.dot(piece, vocab_weight, preferred_element_type=jnp.float32)  15.6 us
    dot_general x1, matrix products, padded_attention(): jnp.einsum('rkgd,rkld->rkgl', queries, key_cache, preferred_element_type=...  10.4 us
    all_gather x1, blocking collectives, shards(): logits = score_rows(lax.all_gather(final, 'dp', axis=0, tiled=True))  9.99 us
    all_gather x1, blocking collectives, shards(): activation = activate(lax.all_gather(feed_in, 'dp', axis=0, tiled=True))  9.81 us
  transfers between devices with their start and end apart: 3, of which 3 were waited for; matrix products, arithmetic and copies ran while one was open for 0% of the time, Pallas kernels for 0%

commit v1 on v0

--- a/solution.py
+++ b/solution.py
@@ -138,7 +138,9 @@
         scatter_dimension=0,
         tiled=True,
     ).astype(jnp.float32)
-    feed = lax.psum(partial_feed.astype(jnp.bfloat16), "mp").astype(jnp.float32)
+    feed = jnp.sum(lax.all_gather(partial_feed.astype(jnp.bfloat16), "mp"), axis=0).astype(
+        jnp.float32
+    )
     residual = (mixed_hidden.astype(jnp.float32) + feed).astype(jnp.bfloat16)
     final = rms_norm(residual, final_gain)
 

time: 246 us -> 222 us (0.902)
  waiting for transfers between devices: 107 us -> 70.2 us
  blocking collectives: 59.2 us -> 73.8 us
    psum x1 -> x0, waiting for transfers between devices: 36.6 us -> none  [shards(): feed = lax.psum(partial_feed.astype(jnp.bfloat16), 'mp').astype(jnp.float32)]
    all_gather x0 -> x1, blocking collectives: none -> 14 us  [shards(): lax.all_gather(partial_feed.astype(jnp.bfloat16), 'mp')]
  transfers between devices with their start and end apart: 3 -> 2, of which waited for: 3 -> 2; matrix products, arithmetic and copies ran while one was open for 0% -> 0% of each run, Pallas kernels for 0% -> 0%
where the time goes in v1:
time: 222 us
  blocking collectives  73.8 us (33%)
  waiting for transfers between devices  70.2 us (32%)
  matrix products  55.7 us (25%)
  between operations  13.6 us (6%)
  other arithmetic  6.8 us (3%)
    unnamed x1, blocking collectives  40 us
    psum x1, waiting for transfers between devices, shards(): lax.psum(partial_heads.astype(jnp.bfloat16), 'mp').astype(jnp.float32)  37.1 us
    reduce_scatter x1, waiting for transfers between devices, shards(): lax.psum_scatter(jnp.dot(lax.slice_in_dim(activation, 0, local_rows * lax...  33.1 us
    dot_general x1, matrix products, score_rows(): return jnp.dot(piece, vocab_weight, preferred_element_type=jnp.float32)  15.6 us
    all_gather x1, blocking collectives, shards(): lax.all_gather(partial_feed.astype(jnp.bfloat16), 'mp')  14 us
    dot_general x1, matrix products, padded_attention(): jnp.einsum('rkgd,rkld->rkgl', queries, key_cache, preferred_element_type=...  10.4 us
    all_gather x1, blocking collectives, shards(): logits = score_rows(lax.all_gather(final, 'dp', axis=0, tiled=True))  10 us
    all_gather x1, blocking collectives, shards(): activation = activate(lax.all_gather(feed_in, 'dp', axis=0, tiled=True))  9.81 us
  transfers between devices with their start and end apart: 2, of which 2 were waited for; matrix products, arithmetic and copies ran while one was open for 0% of the time, Pallas kernels for 0%

profile of v1, /device:TPU:0, one launch (start us, length us, event | category | flops | bytes accessed | tf_op | source)
XLA Modules:
  0.0 221.9 jit_solution(7180133241897645183)
XLA Ops:
  6.5 0.0 all-reduce.6.cloned.1.call-start
  6.6 0.8 convert_element_type.73
  7.4 0.7 iota_compare_fusion.1
  8.1 1.0 fusion.20
  9.1 1.3 convolution_bitcast_fusion.1
  10.4 4.7 %convolution_bitcast_fusion = f32[8,8,128]{2,0,1:T(8,128)S(1)} fusion(bf16[4096,1024]{1,0:T(8,128)(2,1)} %param.21, bf16[8,4096]{1,0:T(8,128)(2,1)} %param.19, f32[4096]{0:T(1024)} %param.20, f32[8]{0:T(128)S(1)} %add_rsqrt_fusion.2), kind=kOutput, calls=%fused_computation.18 | convolution fusion | flops 67239936 | bytes 8503328 | tf_op jit(solution)/shard_map/dot_general | solution.py:95
  15.0 0.1 multiply_cosine_fusion
  15.1 0.1 subtract_convert_fusion.1
  15.2 0.1 subtract_convert_fusion
  15.3 0.1 maximum_bitcast_fusion
  15.4 0.2 fusion.34
  15.6 0.0 copy-start.3
  15.6 10.4 %fusion.43 = (f32[8,2,4]{2,1,0:T(2,128)S(1)}, f32[8,2,4,4096]{3,2,1,0:T(4,128)S(1)}) fusion(bf16[8,2,4096,128]{3,2,1,0:T(8,128)(2,1)} %param.25, bf16[8,2,4,64]{3,2,1,0:T(4,128)(2,1)S(1)} %bitcast.53, bf16[8,2,4,64]{3,2,1,0:T(4,128)(2,1)S(1)} %bitcast.51, pred[8,4096]{1,0:T(8,128)(4,1)S(1)} %iota_compare_fusion.1), kind=kOutput, calls=%fused_computation.79 | convolution fusion | flops 67928000 | bytes 17875200 | tf_op jit(solution)/shard_map/rkgd,rkld->rkgl/dot_general | solution.py:52
  26.0 0.5 fusion.13
  26.6 0.0 copy-done.2
  26.6 2.0 fusion.12
  28.6 7.1 %fusion.10 = bf16[8,2,4,128]{3,2,1,0:T(4,128)(2,1)S(1)} fusion(bf16[8,2,4096,128]{3,2,1,0:T(8,128)(2,1)} %param.26, f32[8,2,4,4096]{3,2,1,0:T(4,128)S(1)} %get-tuple-element.80, f32[8,2,4]{2,1,0:T(2,128)S(1)} %multiply_maximum_fusion, f32[8,2,4]{2,1,0:T(2,128)S(1)} %get-tuple-element.70, f32[8,2,128]{2,1,0:T(2,128)S(1)} %copy.20, ...), kind=kOutput, calls=%fused_computation.19 | convolution fusion | flops 67665920 | bytes 17851136 | tf_op jit(solution)/shard_map/rkgl,rkld->rkgd/dot_general | solution.py:61
  35.7 0.0 copy-start.4
  35.7 5.2 %convolution_convert_fusion.1 = bf16[8,4096]{1,0:T(8,128)(2,1)} fusion(bf16[8,1024]{1,0:T(8,128)(2,1)S(1)} %reshape.136, bf16[1024,4096]{1,0:T(8,128)(2,1)} %param.24), kind=kOutput, calls=%fused_computation.13 | convolution fusion | flops 67141632 | bytes 8470528 | tf_op jit(solution)/shard_map/dot_general | solution.py:116
  40.9 0.0 all-reduce.6.cloned.1.call-update
  40.9 0.0 reduce-scatter.2.cloned.1.call-start
  41.0 37.1 %all-reduce.6.cloned.1.call-done = bf16[8,4096]{1,0:T(8,128)(2,1)} async-done(((bf16[8,4096]{1,0:T(8,128)(2,1)}), bf16[8,4096]{1,0:T(8,128)(2,1)}) %all-reduce.6.cloned.1.call-update) | async-done | bytes 65552 | tf_op jit(solution)/shard_map/psum | solution.py:121
  78.1 1.0 fusion.24
  79.1 0.1 fusion.26
  79.2 9.8 %all_gather.30 = bf16[64,4096]{1,0:T(8,128)(2,1)S(1)} all-gather(bf16[8,4096]{1,0:T(8,128)(2,1)S(1)} %fusion.26), channel_id=1, replica_groups=mesh['dp'=8,'mp'=4] {'dp'}, dimensions={0}, use_global_device_ids=true | all-gather | bytes 589824 | tf_op jit(solution)/shard_map/all_gather | solution.py:130
  89.0 3.2 %fusion.45 = f32[64,448]{1,0:T(8,128)S(1)} fusion(bf16[64,4096]{1,0:T(8,128)(2,1)S(1)} %all_gather.30, bf16[4096,448]{0,1:T(8,128)(2,1)} %param.30), kind=kOutput, calls=%fused_computation.81 | convolution fusion | flops 234881024 | bytes 4308992 | tf_op jit(solution)/shard_map/dot_general | solution.py:126
  92.2 0.0 copy-start.5
  92.2 6.1 %convolution_convert_fusion = bf16[64,4096]{1,0:T(8,128)(2,1)} fusion(bf16[448,4096]{1,0:T(8,128)(2,1)} %param.32, bf16[64,4096]{1,0:T(8,128)(2,1)S(1)} %all_gather.30, bf16[4096,448]{0,1:T(8,128)(2,1)} %param.31, f32[64,448]{1,0:T(8,128)S(1)} %fusion.45), kind=kOutput, calls=%fused_computation.12 | convolution fusion | flops 470196224 | bytes 8503296 | tf_op jit(solution)/shard_map/dot_general | solution.py:132
  98.3 0.0 reduce-scatter.2.cloned.1.call-update
  98.4 33.1 %reduce-scatter.2.cloned.1.call-done = bf16[8,4096]{1,0:T(8,128)(2,1)} async-done(((bf16[64,4096]{1,0:T(8,128)(2,1)}), bf16[8,4096]{1,0:T(8,128)(2,1)}) %reduce-scatter.2.cloned.1.call-update) | async-done | bytes 65552 | tf_op jit(solution)/shard_map/reduce_scatter | solution.py:131
  131.4 14.0 %all-gather = bf16[32,4096]{1,0:T(8,128)(2,1)S(1)} all-gather(bf16[8,4096]{1,0:T(8,128)(2,1)} %reduce-scatter.2.cloned.1.call-done), channel_id=2, replica_groups=mesh['dp'=8,'mp'=4] {'mp'}, dimensions={0}, use_global_device_ids=true | all-gather | bytes 327680 | tf_op jit(solution)/shard_map/all_gather | solution.py:141
  145.5 0.1 fusion.17
  145.7 0.1 fusion.19
  145.8 10.0 %all_gather.33 = bf16[64,4096]{1,0:T(8,128)(2,1)S(1)} all-gather(bf16[8,4096]{1,0:T(8,128)(2,1)S(1)} %fusion.19), channel_id=1, replica_groups=mesh['dp'=8,'mp'=4] {'dp'}, dimensions={0}, use_global_device_ids=true | all-gather | bytes 589824 | tf_op jit(solution)/shard_map/all_gather | solution.py:150
  155.8 15.6 %fusion.44 = (f32[64]{0:T(128)S(1)}, f32[64,4008]{1,0:T(8,128)S(1)}) fusion(bf16[64,4096]{1,0:T(8,128)(2,1)S(1)} %all_gather.33, bf16[4096,4008]{0,1:T(8,128)(2,1)} %param.34), kind=kOutput, calls=%fused_computation.80 | convolution fusion | flops 2101602816 | bytes 34384128 | tf_op jit(solution)/shard_map/dot_general | solution.py:148
  171.4 0.5 select_reduce_fusion
  171.8 0.3 dynamic-update-slice
  172.1 0.3 dynamic-update-slice.2
  172.4 0.3 dynamic-update-slice.1
  172.6 40.0 %all-reduce.3 = (f32[2048]{0:T(1024)S(1)}, f32[2048]{0:T(1024)S(1)}, f32[2048]{0:T(1024)S(1)}) all-reduce(f32[2048]{0:T(1024)S(1)} %dynamic-update-slice, f32[2048]{0:T(1024)S(1)} %dynamic-update-slice.1, f32[2048]{0:T(1024)S(1)} %dynamic-update-slice.2), channel_id=3, replica_groups=mesh['dp'=8,'mp'=4] {'dp','mp'}, use_global_device_ids=true, to_apply=%add | all-reduce | flops 6144 | bytes 49152
  212.6 0.1 slice.53
  212.7 0.1 slice.54
  212.8 0.1 slice.55
  212.8 0.1 reshape.148
  212.9 0.1 reshape.149
  213.0 0.1 reshape.150
  213.0 1.4 while.14
  214.4 0.6 compare_select_fusion
  (62 shorter events, 1.1 us)
Async XLA Ops:
  6.5 2.6 %copy-start = (bf16[4096,256]{1,0:T(8,128)(2,1)S(1)}, bf16[4096,256]{1,0:T(8,128)(2,1)}, u32[]{:S(2)}) copy-start(bf16[4096,256]{1,0:T(8,128)(2,1)} %param.22) | copy-start | bytes 6291460
  6.5 71.6 %all-reduce.6.cloned.1.call-start = ((), (), s32[]{:S(2)}) async-start(), calls=%async_computation.1 | async-start | bytes 131072 | tf_op jit(solution)/shard_map/psum | solution.py:121
  15.6 10.9 %copy-start.2 = (bf16[8,4096]{1,0:T(8,128)(2,1)S(1)}, bf16[8,4096]{1,0:T(8,128)(2,1)}, u32[]{:S(2)}) copy-start(bf16[8,4096]{1,0:T(8,128)(2,1)} %param.19) | copy-start | bytes 196612
  15.6 10.9 %copy-start.3 = (f32[4096]{0:T(1024)S(1)}, f32[4096]{0:T(1024)}, u32[]{:S(2)}) copy-start(f32[4096]{0:T(1024)} %param.20) | copy-start | bytes 49156
  35.7 43.4 %copy-start.4 = (f32[4096]{0:T(1024)S(1)}, f32[4096]{0:T(1024)}, u32[]{:S(2)}) copy-start(f32[4096]{0:T(1024)} %param.29) | copy-start | bytes 49156
  40.9 90.5 %reduce-scatter.2.cloned.1.call-start = ((), (), s32[]{:S(2)}) async-start(), calls=%async_computation.2 | async-start | bytes 589824 | tf_op jit(solution)/shard_map/reduce_scatter | solution.py:131
  92.2 6.1 %copy-start.7 = (s32[64]{0:T(128)S(1)}, s32[64]{0:T(128)}, u32[]{:S(2)}) copy-start(s32[64]{0:T(128)} %param.35) | copy-start | bytes 772
  92.2 53.4 %copy-start.5 = (f32[4096]{0:T(1024)S(1)}, f32[4096]{0:T(1024)}, u32[]{:S(2)}) copy-start(f32[4096]{0:T(1024)} %param.33) | copy-start | bytes 49156
  155.8 58.7 %copy-start.6 = (s32[8]{0:T(128)S(1)}, s32[8]{0:T(128)}, u32[]{:S(2)}) copy-start(s32[8]{0:T(128)} %param.28) | copy-start | bytes 100
  155.8 59.3 %copy-start.1 = (bf16[4096,256]{1,0:T(8,128)(2,1)S(1)}, bf16[4096,256]{1,0:T(8,128)(2,1)}, u32[]{:S(2)}) copy-start(bf16[4096,256]{1,0:T(8,128)(2,1)} %param.22) | copy-start | bytes 6291460
Sparse Core Ops, SparseCore 0:
  41.1 37.0 all-reduce.5
  98.5 32.9 reduce-scatter.1
